TPU v7x, 128 devices: a whole 4x4x4 slice. The times are simulated.
128 devices in a mesh: bank: 8 (over x, core), lane: 16 (over z, y).
Axes of the slice: x: 4, y: 4, z: 4, core: 2. Of those that a mesh axis runs over, the one named last changes fastest.
Arguments:
- amplitudes: float32 [2, 2048, 128, 128], P(None, ('bank', 'lane')), may hold values from -6 to 6
- energies: float32 [2048, 128, 128], P(('bank', 'lane')), may hold values from -2 to 2
- diagonal_angles: float32 [2, 128], replicated, may hold values from 0.3 to 1.2
- turn_angles: float32 [2, 4], replicated, may hold values from 0.3 to 1.2
Outputs:
- state_after: float32 [2, 2048, 128, 128], P(None, ('bank', 'lane'))
All inputs are finite; a program needn't handle non-finite values.
Results may differ from a plain program's by a relative error of at most 0.0003.
Values sent between devices are 32-bit elements; how exact they have to be, the bound alone decides.
A program may use at most 64 MiB of HBM per device.

v0:
```python
import jax
import jax.numpy as jnp
from jax import lax
from jax.sharding import Mesh
from jax.sharding import PartitionSpec as P

LAYERS = 2
BANK = ("bank_0", "bank_1")
BANK_LANE = ("bank_0", "bank_1", "lane")


def split_up(shard, dim, peers):
    before, after = (shard.shape[:dim], shard.shape[dim + 1 :])
    return jnp.moveaxis(shard.reshape(*before, peers, -1, *after), dim, 0)


def in_order(tiles, dim):
    lengths = list(tiles.shape[1:])
    lengths[dim] *= tiles.shape[0]
    return jnp.moveaxis(tiles, 0, dim).reshape(lengths)


def moved_by_axis(tiles, axes, order):
    inside = tiles.shape[1:]
    filled = tiles.reshape(*(lax.axis_size(a) for a in axes), *inside)
    for k in order:
        filled = lax.all_to_all(filled, axes[k], k, k, tiled=True)
    return filled.reshape(-1, *inside)


def core_and_chips(shard, groups, order, split_dim, concat_dim):
    peers = lax.axis_size(groups[0]) * lax.axis_size(groups[1])
    tiles = split_up(shard, split_dim, peers)
    return in_order(moved_by_axis(tiles, groups, order), concat_dim)


def count_bits(values, count):
    places = jnp.arange(count.bit_length() - 1, dtype=jnp.int32)
    return jnp.sum(values[..., None] >> places & 1, axis=-1)


def plane_table(count, angle):
    rank = jnp.arange(count, dtype=jnp.int32)
    apart = count_bits(rank[:, None] ^ rank[None, :], count)
    minus = count_bits(rank[:, None] & (rank[:, None] ^ rank[None, :]), count)
    bits = count.bit_length() - 1
    size = jnp.cos(angle) ** (bits - apart).astype(jnp.float32) * jnp.sin(angle) ** apart.astype(
        jnp.float32
    )
    return size * jnp.where(minus % 2 == 1, -1.0, 1.0).astype(jnp.float32)


def mix_dim(values, dim, angle):
    real_part = plane_table(values.shape[dim], angle)
    moved = jnp.tensordot(values, real_part, axes=([dim], [0]), precision=lax.Precision.HIGHEST)
    return jnp.moveaxis(moved, -1, dim)


def phase_step(values, levels, angle):
    turn = angle * levels
    return jnp.stack(
        [
            values[0] * jnp.cos(turn) + values[1] * jnp.sin(turn),
            values[1] * jnp.cos(turn) - values[0] * jnp.sin(turn),
        ]
    )


def body(amplitudes, energies, diagonal_angles, turn_angles):
    values = amplitudes
    for layer in range(LAYERS):
        values = phase_step(values, energies, diagonal_angles[layer])
        values = mix_dim(values, 3, turn_angles[layer, 0])
        values = mix_dim(values, 2, turn_angles[layer, 1])
        moved = lax.all_to_all(values, BANK, split_axis=2, concat_axis=1, tiled=True)
        moved = mix_dim(moved, 1, turn_angles[layer, 2])
        values = core_and_chips(moved, ("bank_0", "bank_1"), (1, 0), 1, 2)
        moved = lax.all_to_all(values, "lane", split_axis=3, concat_axis=1, tiled=True)
        spread = moved.reshape(2, lax.axis_size("lane"), -1, moved.shape[2], moved.shape[3])
        moved = mix_dim(spread, 1, turn_angles[layer, 3]).reshape(moved.shape)
        values = lax.all_to_all(moved, "lane", split_axis=1, concat_axis=3, tiled=True)
    return values


def solution(mesh):
    torus = Mesh(mesh.devices.reshape(4, 2, mesh.shape["lane"]), ("bank_0", "bank_1", "lane"))
    in_specs = (P(None, BANK_LANE, None, None), P(BANK_LANE, None, None), P(), P())
    out_specs = P(None, BANK_LANE, None, None)
    return jax.shard_map(body, mesh=torus, in_specs=in_specs, out_specs=out_specs, check_vma=False)
```

profile of v0, /device:TPU:1, one launch (start us, length us, event | category | flops | bytes accessed | tf_op | source)
XLA Modules:
  0.0 325.4 jit_solution(13171402460288628376)
XLA Ops:
  0.0 1.6 fusion.163
  4.7 0.8 slice_bitcast_fusion
  5.5 5.2 %fusion.21 = (f32[1,16,128,128]{3,2,1,0:T(8,128)S(1)}, f32[1,16,128,128]{3,2,1,0:T(8,128)S(1)}) fusion(f32[2,16,128,128]{3,2,1,0:T(8,128)} %param.4, f32[16,128,128]{2,1,0:T(8,128)} %param.5, f32[128]{0:T(128)S(1)} %get-tuple-element.20), kind=kLoop, calls=%fused_computation.22 | loop fusion | flops 1835008 | bytes 5243392 | tf_op jit(solution)/shard_map/stack | solution.py:61
  10.7 2.3 fusion
  12.9 2.0 convolution_bitcast_fusion.1
  14.9 2.0 copy.105
  16.9 5.8 %all-to-all-start = ((f32[2,16,128,128]{3,1,0,2:T(8,128)}), f32[2,16,128,128]{3,1,0,2:T(8,128)S(1)}, u32[]{:S(2)}, u32[]{:S(2)}) async-start(f32[2,16,128,128]{3,1,0,2:T(8,128)} %copy.105), calls=%async_computation | async-start | bytes 4194304 | tf_op jit(solution)/shard_map/all_to_all | solution.py:75
  24.1 24.8 %all-to-all-done = f32[2,16,128,128]{3,1,0,2:T(8,128)S(1)} async-done(((f32[2,16,128,128]{3,1,0,2:T(8,128)}), f32[2,16,128,128]{3,1,0,2:T(8,128)S(1)}, u32[]{:S(2)}, u32[]{:S(2)}) %all-to-all-start) | async-done | bytes 2097184 | tf_op jit(solution)/shard_map/all_to_all | solution.py:75
  48.9 0.2 copy.107
  49.1 2.2 fusion.31
  51.3 1.2 copy.110
  52.5 6.0 %all_to_all.119 = f32[4,2,2,16,16,128]{5,4,0,3,2,1:T(8,128)S(1)} all-to-all(f32[4,2,2,16,16,128]{5,4,0,3,2,1:T(8,128)S(1)} %copy.110), channel_id=1, replica_groups=mesh['bank_0'=4,'bank_1'=2,'lane'=16] {'bank_1'}, dimensions={1} | all-to-all | bytes 4194304 | tf_op jit(solution)/shard_map/all_to_all | solution.py:27
  58.6 0.3 copy.111
  58.9 28.5 %all_to_all.120 = f32[4,2,2,16,16,128]{5,4,1,3,2,0:T(8,128)S(1)} all-to-all(f32[4,2,2,16,16,128]{5,4,1,3,2,0:T(8,128)S(1)} %copy.111), channel_id=1, replica_groups=mesh['bank_0'=4,'bank_1'=2,'lane'=16] {'bank_0'}, dimensions={0} | all-to-all | bytes 4194304 | tf_op jit(solution)/shard_map/all_to_all | solution.py:27
  87.4 0.2 copy.112
  87.6 2.0 copy.113
  89.5 7.8 %all-to-all-start.3 = ((f32[2,16,128,128]{2,1,0,3:T(8,128)}), f32[2,16,128,128]{2,1,0,3:T(8,128)S(1)}, u32[]{:S(2)}, u32[]{:S(2)}) async-start(f32[2,16,128,128]{2,1,0,3:T(8,128)} %copy.113), calls=%async_computation.3 | async-start | bytes 4194304 | tf_op jit(solution)/shard_map/all_to_all | solution.py:78
  98.9 27.5 %all-to-all-done.3 = f32[2,16,128,128]{2,1,0,3:T(8,128)S(1)} async-done(((f32[2,16,128,128]{2,1,0,3:T(8,128)}), f32[2,16,128,128]{2,1,0,3:T(8,128)S(1)}, u32[]{:S(2)}, u32[]{:S(2)}) %all-to-all-start.3) | async-done | bytes 2097184 | tf_op jit(solution)/shard_map/all_to_all | solution.py:78
  126.4 3.6 %fusion.14 = f32[2,16,16,128,8]{3,1,4,2,0:T(8,128)S(1)} fusion(f32[2,16,128,16,8]{2,1,0,4,3:T(8,128)S(1)} %bitcast.151, s32[16,16]{1,0:T(8,128)S(1)} %get-tuple-element.22, f32[]{:T(128)} %bitcast.32, f32[]{:T(128)} %bitcast.31, s32[16,16]{1,0:T(8,128)S(1)} %get-tuple-element.21), kind=kOutput, calls=%fused_computation.15 | convolution fusion | flops 100667904 | bytes 4196360 | tf_op jit(solution)/shard_map/dot_general | solution.py:55
  130.0 0.6 copy.117
  130.6 1.5 copy.118
  132.1 5.2 %all-to-all-start.4 = ((f32[2,256,128,8]{2,3,0,1:T(8,128)}), f32[2,256,128,8]{2,3,0,1:T(8,128)S(1)}, u32[]{:S(2)}, u32[]{:S(2)}) async-start(f32[2,256,128,8]{2,3,0,1:T(8,128)} %copy.118), calls=%async_computation.4 | async-start | bytes 4194304 | tf_op jit(solution)/shard_map/all_to_all | solution.py:81
  140.1 27.1 %all-to-all-done.4 = f32[2,256,128,8]{2,3,0,1:T(8,128)S(1)} async-done(((f32[2,256,128,8]{2,3,0,1:T(8,128)}), f32[2,256,128,8]{2,3,0,1:T(8,128)S(1)}, u32[]{:S(2)}, u32[]{:S(2)}) %all-to-all-start.4) | async-done | bytes 2097184 | tf_op jit(solution)/shard_map/all_to_all | solution.py:81
  167.3 0.2 fusion.162
  167.6 0.3 copy.121
  168.1 0.3 copy.123
  168.4 6.2 %add_bitcast_fusion = (f32[1,16,128,128]{3,2,1,0:T(8,128)S(1)}, f32[1,16,128,128]{3,2,1,0:T(8,128)S(1)}) fusion(f32[16,128,128]{2,1,0:T(8,128)S(1)} %copy.123, f32[16,128,128]{2,1,0:T(8,128)S(1)} %copy.121, f32[16,128,128]{2,1,0:T(8,128)} %param.5, f32[128]{0:T(128)S(1)} %get-tuple-element.19), kind=kLoop, calls=%fused_computation.30 | loop fusion | flops 1835008 | bytes 5243392 | tf_op jit(solution)/shard_map/stack | solution.py:61
  174.6 2.3 fusion.4
  176.8 2.0 convolution_bitcast_fusion
  178.8 2.0 copy.127
  180.8 5.9 %all-to-all-start.5 = ((f32[2,16,128,128]{3,1,0,2:T(8,128)}), f32[2,16,128,128]{3,1,0,2:T(8,128)S(1)}, u32[]{:S(2)}, u32[]{:S(2)}) async-start(f32[2,16,128,128]{3,1,0,2:T(8,128)} %copy.127), calls=%async_computation.5 | async-start | bytes 4194304 | tf_op jit(solution)/shard_map/all_to_all | solution.py:75
  188.0 25.0 %all-to-all-done.5 = f32[2,16,128,128]{3,1,0,2:T(8,128)S(1)} async-done(((f32[2,16,128,128]{3,1,0,2:T(8,128)}), f32[2,16,128,128]{3,1,0,2:T(8,128)S(1)}, u32[]{:S(2)}, u32[]{:S(2)}) %all-to-all-start.5) | async-done | bytes 2097184 | tf_op jit(solution)/shard_map/all_to_all | solution.py:75
  212.9 0.2 copy.129
  213.2 2.2 fusion.38
  215.4 1.2 copy.132
  216.6 6.0 %all_to_all.121 = f32[4,2,2,16,16,128]{5,4,0,3,2,1:T(8,128)S(1)} all-to-all(f32[4,2,2,16,16,128]{5,4,0,3,2,1:T(8,128)S(1)} %copy.132), channel_id=1, replica_groups=mesh['bank_0'=4,'bank_1'=2,'lane'=16] {'bank_1'}, dimensions={1} | all-to-all | bytes 4194304 | tf_op jit(solution)/shard_map/all_to_all | solution.py:27
  222.6 0.3 copy.133
  222.9 28.5 %all_to_all.122 = f32[4,2,2,16,16,128]{5,4,1,3,2,0:T(8,128)S(1)} all-to-all(f32[4,2,2,16,16,128]{5,4,1,3,2,0:T(8,128)S(1)} %copy.133), channel_id=1, replica_groups=mesh['bank_0'=4,'bank_1'=2,'lane'=16] {'bank_0'}, dimensions={0} | all-to-all | bytes 4194304 | tf_op jit(solution)/shard_map/all_to_all | solution.py:27
  251.4 0.2 copy.134
  251.6 2.0 copy.135
  253.6 3.7 %all-to-all-start.8 = ((f32[2,16,128,128]{2,1,0,3:T(8,128)}), f32[2,16,128,128]{2,1,0,3:T(8,128)S(1)}, u32[]{:S(2)}, u32[]{:S(2)}) async-start(f32[2,16,128,128]{2,1,0,3:T(8,128)} %copy.135), calls=%async_computation.8 | async-start | bytes 4194304 | tf_op jit(solution)/shard_map/all_to_all | solution.py:78
  258.7 28.5 %all-to-all-done.8 = f32[2,16,128,128]{2,1,0,3:T(8,128)S(1)} async-done(((f32[2,16,128,128]{2,1,0,3:T(8,128)}), f32[2,16,128,128]{2,1,0,3:T(8,128)S(1)}, u32[]{:S(2)}, u32[]{:S(2)}) %all-to-all-start.8) | async-done | bytes 2097184 | tf_op jit(solution)/shard_map/all_to_all | solution.py:78
  287.2 3.6 %fusion.17 = f32[2,16,16,128,8]{3,1,4,2,0:T(8,128)S(1)} fusion(f32[2,16,128,16,8]{2,1,0,4,3:T(8,128)S(1)} %bitcast.152, s32[16,16]{1,0:T(8,128)S(1)} %get-tuple-element.22, f32[]{:T(128)} %bitcast.71, f32[]{:T(128)} %bitcast.70, s32[16,16]{1,0:T(8,128)S(1)} %get-tuple-element.21), kind=kOutput, calls=%fused_computation.16 | convolution fusion | flops 100667904 | bytes 4196360 | tf_op jit(solution)/shard_map/dot_general | solution.py:55
  290.8 0.6 copy.139
  291.4 0.2 copy.140
  291.6 31.8 %all_to_all.123 = f32[2,256,128,8]{2,3,0,1:T(8,128)S(1)} all-to-all(f32[2,256,128,8]{2,3,0,1:T(8,128)S(1)} %copy.140), channel_id=1, replica_groups=mesh['bank_0'=4,'bank_1'=2,'lane'=16] {'lane'}, dimensions={1} | all-to-all | bytes 4194304 | tf_op jit(solution)/shard_map/all_to_all | solution.py:81
  323.4 0.2 copy.182
  323.6 1.8 copy.143
  (11 shorter events, 0.5 us)
Async XLA Ops:
  16.9 32.0 %all-to-all-start = ((f32[2,16,128,128]{3,1,0,2:T(8,128)}), f32[2,16,128,128]{3,1,0,2:T(8,128)S(1)}, u32[]{:S(2)}, u32[]{:S(2)}) async-start(f32[2,16,128,128]{3,1,0,2:T(8,128)} %copy.105), calls=%async_computation | async-start | bytes 4194304 | tf_op jit(solution)/shard_map/all_to_all | solution.py:75
  89.5 36.9 %all-to-all-start.3 = ((f32[2,16,128,128]{2,1,0,3:T(8,128)}), f32[2,16,128,128]{2,1,0,3:T(8,128)S(1)}, u32[]{:S(2)}, u32[]{:S(2)}) async-start(f32[2,16,128,128]{2,1,0,3:T(8,128)} %copy.113), calls=%async_computation.3 | async-start | bytes 4194304 | tf_op jit(solution)/shard_map/all_to_all | solution.py:78
  132.1 35.1 %all-to-all-start.4 = ((f32[2,256,128,8]{2,3,0,1:T(8,128)}), f32[2,256,128,8]{2,3,0,1:T(8,128)S(1)}, u32[]{:S(2)}, u32[]{:S(2)}) async-start(f32[2,256,128,8]{2,3,0,1:T(8,128)} %copy.118), calls=%async_computation.4 | async-start | bytes 4194304 | tf_op jit(solution)/shard_map/all_to_all | solution.py:81
  180.8 32.1 %all-to-all-start.5 = ((f32[2,16,128,128]{3,1,0,2:T(8,128)}), f32[2,16,128,128]{3,1,0,2:T(8,128)S(1)}, u32[]{:S(2)}, u32[]{:S(2)}) async-start(f32[2,16,128,128]{3,1,0,2:T(8,128)} %copy.127), calls=%async_computation.5 | async-start | bytes 4194304 | tf_op jit(solution)/shard_map/all_to_all | solution.py:75
  253.6 33.6 %all-to-all-start.8 = ((f32[2,16,128,128]{2,1,0,3:T(8,128)}), f32[2,16,128,128]{2,1,0,3:T(8,128)S(1)}, u32[]{:S(2)}, u32[]{:S(2)}) async-start(f32[2,16,128,128]{2,1,0,3:T(8,128)} %copy.135), calls=%async_computation.8 | async-start | bytes 4194304 | tf_op jit(solution)/shard_map/all_to_all | solution.py:78
where the time goes:
time: 327 us; the launch traced here: 325 us
  waiting for transfers between devices  133 us (41%)
  blocking collectives  101 us (31%)
  starting transfers between devices  28.4 us (9%)
  local copies, waits for them, and re-layouts  20.3 us (6%)
  matrix products  20 us (6%)
  other arithmetic  11.5 us (4%)
  between operations  11.5 us (4%)
    all_to_all x4, blocking collectives, moved_by_axis(): filled = lax.all_to_all(filled, axes[k], k, k, tiled=True)  69.1 us
    all_to_all x2, waiting for transfers between devices, body(): lax.all_to_all(values, 'lane', split_axis=3, concat_axis=1, tiled=True)  56 us
    all_to_all x2, waiting for transfers between devices, body(): lax.all_to_all(values, BANK, split_axis=2, concat_axis=1, tiled=True)  49.8 us
    all_to_all x1, blocking collectives, body(): lax.all_to_all(moved, 'lane', split_axis=1, concat_axis=3, tiled=True)  31.8 us
    all_to_all x1, waiting for transfers between devices, body(): lax.all_to_all(moved, 'lane', split_axis=1, concat_axis=3, tiled=True)  27.1 us
    dot_general x8, matrix products, mix_dim(): jnp.tensordot(values, real_part, axes=([dim], [0]), precision=lax.Precisi...  20 us
    all_to_all x2, starting transfers between devices, body(): lax.all_to_all(values, BANK, split_axis=2, concat_axis=1, tiled=True)  11.7 us
    all_to_all x2, starting transfers between devices, body(): lax.all_to_all(values, 'lane', split_axis=3, concat_axis=1, tiled=True)  11.5 us
  transfers between devices with their start and end apart: 5, of which 5 were waited for; matrix products, arithmetic and copies ran while one was open for 0% of the time, Pallas kernels for 0%

commit v1 on v0

v1 whole, which is shorter than its diff:
```python
import functools

import jax
import jax.numpy as jnp
from jax import lax
from jax.experimental import pallas as pl
from jax.experimental.pallas import tpu as pltpu
from jax.sharding import PartitionSpec as P

N_DEV = 128
N_LANE = 16
BITS = 7


def place():
    return lax.axis_index("bank"), lax.axis_index("lane")


def partner(step):
    bank, lane = place()
    step = lax.rem(step * 37, N_DEV)
    x = lax.rem(bank // 2 + step // 32, 4)
    core = lax.rem(lax.rem(bank, 2) + lax.rem(step // 16, 2), 2)
    z = lax.rem(lane // 4 + lax.rem(step // 4, 4), 4)
    y = lax.rem(lax.rem(lane, 4) + lax.rem(step, 4), 4)
    to_bank = x * 2 + core
    to_lane = z * 4 + y
    return (to_bank, to_lane), to_bank * N_LANE + to_lane


def send_all(pick_src, pick_dst, send_sem, recv_sem):
    bank, lane = place()
    me = bank * N_LANE + lane

    def one(step, carry):
        device, index = partner(step)
        pltpu.make_async_remote_copy(
            src_ref=pick_src(index),
            dst_ref=pick_dst(me),
            send_sem=send_sem,
            recv_sem=recv_sem,
            device_id=device,
            device_id_type=pl.DeviceIdType.MESH,
        ).start()
        return carry

    lax.fori_loop(1, N_DEV, one, 0)


def wait_bytes(ref, sem):
    pltpu.make_async_copy(ref, ref, sem).wait()


def cos_sin(half):
    sq = half * half
    s = 1.0 / 6227020800.0
    for term in (-1.0 / 39916800.0, 1.0 / 362880.0, -1.0 / 5040.0, 1.0 / 120.0, -1.0 / 6.0):
        s = s * sq + term
    s = half + half * (sq * s)
    c = 1.0 / 479001600.0
    for term in (-1.0 / 3628800.0, 1.0 / 40320.0, -1.0 / 720.0, 1.0 / 24.0, -0.5):
        c = c * sq + term
    c = 1.0 + sq * c
    twice = s + s
    return 1.0 - twice * s, twice * c


def butterfly(tiles, tan):
    tiles = list(tiles)
    step = 1
    while step < len(tiles):
        for i in range(len(tiles)):
            if i & step:
                continue
            u, v = tiles[i], tiles[i + step]
            tiles[i] = u - tan * v
            tiles[i + step] = v + tan * u
        step *= 2
    return tiles


def rotate_phase(re, im, half):
    c, s = cos_sin(half)
    return re * c + im * s, im * c - re * s


def sublane_mix(values, tan):
    place_in = lax.broadcasted_iota(jnp.int32, values.shape, 1)
    for step in (4, 2, 1):
        upper = (place_in // step) % 2 == 1
        below = pltpu.roll(values, step, 1)
        other = below if step == 4 else jnp.where(upper, below, pltpu.roll(values, 8 - step, 1))
        values = values + jnp.where(upper, tan, -tan) * other
    return values


def lane_table(cos, sin, scale):
    row = lax.broadcasted_iota(jnp.int32, (128, 128), 0)
    col = lax.broadcasted_iota(jnp.int32, (128, 128), 1)
    table = jnp.broadcast_to(scale, (128, 128))
    for bit in range(BITS):
        r = (row // 2**bit) % 2
        c = (col // 2**bit) % 2
        table = table * jnp.where(r == c, cos, jnp.where(r > c, -sin, sin))
    high = table.astype(jnp.bfloat16)
    low = (table - high.astype(jnp.float32)).astype(jnp.bfloat16)
    both = jnp.concatenate([high, low], axis=1)
    return jnp.concatenate([both, both], axis=0)


def lane_mix(values, table):
    high = values.astype(jnp.bfloat16)
    low = (values - high.astype(jnp.float32)).astype(jnp.bfloat16)
    parts = jnp.concatenate([high, low], axis=1)
    out = jnp.dot(parts, table, preferred_element_type=jnp.float32)
    return out[:, :128] + out[:, 128:]


def kernel(amp, energy, diag, turn, out, a_in, e_in, e_rx, fwd, mid, back, fin, tables, tans, sems, sends, recvs):
    bank, lane = place()
    me = bank * N_LANE + lane

    get_e = pltpu.make_async_copy(energy, e_in, sems.at[0])
    get_a = pltpu.make_async_copy(amp, a_in, sems.at[1])
    get_e.start()
    get_a.start()

    cos, sin = cos_sin(turn[...] * 0.5)
    tan = sin / cos
    for layer in range(2):
        for group in range(4):
            tans[layer, group] = jnp.broadcast_to(tan[layer : layer + 1, group : group + 1], (8, 128))
        c = [cos[layer : layer + 1, g : g + 1] for g in range(4)]
        c12 = c[1] * c[2]
        c12_2 = c12 * c12
        c3_2 = c[3] * c[3]
        scale = c12_2 * c12_2 * c12_2 * c12 * c3_2 * c3_2
        tables[layer] = lane_table(c[0], sin[layer : layer + 1, 0:1], scale)

    get_e.wait()
    send_all(lambda i: e_in.at[i], lambda i: e_rx.at[i], sends.at[0], recvs.at[0])
    get_a.wait()
    e_rx[me] = e_in[me]

    def first(i, carry):
        at = pl.ds(i * 8, 8)
        half = e_in[at] * (diag[0:1, :] * 0.5).reshape(1, 1, 1, 128)
        re, im = rotate_phase(a_in[0, at], a_in[1, at], half)
        values = jnp.concatenate([re, im], axis=0)
        mixed = lane_mix(values.reshape(256, 128), tables[0]).reshape(32, 8, 128)
        mixed = sublane_mix(mixed, tans[0, 1, 0:1, :].reshape(1, 1, 128))
        mixed = mixed.reshape(2, 16, 8, 128)
        tan1 = tans[0, 1]
        for part in range(2):
            tiles = butterfly([mixed[part, j] for j in range(16)], tan1)
            for j in range(16):
                a_in[part, i * 8 + j // 2, j % 2] = tiles[j]
        return carry

    lax.fori_loop(0, 16, first, 0)

    tan2 = tans[0, 2]
    for k in range(2):

        def blocks(i, carry):
            part, row = i // 8, lax.rem(i, 8)
            tiles = butterfly([a_in[part, b * 8 + row, k] for b in range(16)], tan2)
            for b in range(16):
                fwd[k, b * 8 + row, part] = tiles[b]
            return carry

        lax.fori_loop(0, 16, blocks, 0)
        send_all(
            lambda i: fwd.at[k, i], lambda i: mid.at[k, i], sends.at[1 + k], recvs.at[1 + k]
        )
        mid[k, me] = fwd[k, me]

    wait_bytes(e_rx.at[pl.ds(0, N_DEV - 1)], recvs.at[0])
    for k in range(2):
        wait_bytes(mid.at[k, pl.ds(0, N_DEV - 1)], recvs.at[1 + k])

        def lanes_1(i, carry):
            b, part = i // 2, lax.rem(i, 2)
            tiles = butterfly([mid[k, b * 16 + l, part] for l in range(16)], tans[0, 3])
            for l in range(16):
                mid[k, b * 16 + l, part] = tiles[l]
            return carry

        lax.fori_loop(0, 16, lanes_1, 0)

        def banks(l, carry):
            re = butterfly([mid[k, b * 16 + l, 0] for b in range(8)], tans[0, 2])
            im = butterfly([mid[k, b * 16 + l, 1] for b in range(8)], tans[0, 2])
            angle = diag[1:2, :] * 0.5
            for b in range(8):
                re[b], im[b] = rotate_phase(re[b], im[b], e_rx[b * 16 + l, k] * angle)
            re = butterfly(re, tans[1, 2])
            im = butterfly(im, tans[1, 2])
            for b in range(8):
                mid[k, b * 16 + l, 0] = re[b]
                mid[k, b * 16 + l, 1] = im[b]
            return carry

        lax.fori_loop(0, 16, banks, 0)

        def lanes_2(b, carry):
            both = []
            for part in range(2):
                tiles = butterfly([mid[k, b * 16 + l, part] for l in range(16)], tans[1, 3])
                both.append(jnp.stack(tiles))
            values = jnp.stack(both).reshape(256, 128)
            mixed = lane_mix(values, tables[1]).reshape(32, 8, 128)
            mixed = sublane_mix(mixed, tans[1, 1, 0:1, :].reshape(1, 1, 128))
            mixed = mixed.reshape(2, 16, 8, 128)
            for part in range(2):
                back[k, part, pl.ds(b * 16, 16)] = mixed[part]
            return carry

        lax.fori_loop(0, 8, lanes_2, 0)
        for part in range(2):
            n = 3 + 2 * k + part
            send_all(
                lambda i: back.at[k, part, i], lambda i: fin.at[k, part, i], sends.at[n], recvs.at[n]
            )
            fin[k, part, me] = back[k, part, me]

    for k in range(2):
        for part in range(2):
            n = 3 + 2 * k + part
            wait_bytes(fin.at[k, part, pl.ds(0, N_DEV - 1)], recvs.at[n])

            def rows(b, carry):
                tiles = butterfly([fin[k, part, b * 8 + r] for r in range(8)], tans[1, 1])
                for r in range(8):
                    fin[k, part, b * 8 + r] = tiles[r]
                return carry

            lax.fori_loop(0, 16, rows, 0)

            def last(r, carry):
                tiles = butterfly([fin[k, part, b * 8 + r] for b in range(16)], tans[1, 2])
                if k == 0:
                    for b in range(16):
                        fin[0, part, b * 8 + r] = tiles[b]
                else:
                    t = tans[1, 1]
                    for b in range(16):
                        u = fin[0, part, b * 8 + r]
                        v = tiles[b]
                        a_in[part, b * 8 + r, 0] = u - t * v
                        a_in[part, b * 8 + r, 1] = v + t * u
                return carry

            lax.fori_loop(0, 8, last, 0)
            if k == 1:
                pltpu.make_async_copy(a_in.at[part], out.at[part], sems.at[part]).start()
    for part in range(2):
        pltpu.make_async_copy(a_in.at[part], out.at[part], sems.at[part]).wait()

    wait_bytes(e_in.at[pl.ds(0, N_DEV - 1)], sends.at[0])
    for k in range(2):
        wait_bytes(fwd.at[k, pl.ds(0, N_DEV - 1)], sends.at[1 + k])
        for part in range(2):
            wait_bytes(back.at[k, part, pl.ds(0, N_DEV - 1)], sends.at[3 + 2 * k + part])


def body(amplitudes, energies, diagonal_angles, turn_angles):
    f32 = jnp.float32
    anywhere = pl.BlockSpec(memory_space=pl.ANY)
    vmem = pl.BlockSpec(memory_space=pltpu.VMEM)
    out = pl.pallas_call(
        kernel,
        out_shape=jax.ShapeDtypeStruct((2, N_DEV, 2, 8, 128), f32),
        in_specs=[anywhere, anywhere, vmem, vmem],
        out_specs=anywhere,
        scratch_shapes=[
            pltpu.VMEM((2, N_DEV, 2, 8, 128), f32),
            pltpu.VMEM((N_DEV, 2, 8, 128), f32),
            pltpu.VMEM((N_DEV, 2, 8, 128), f32),
            pltpu.VMEM((2, N_DEV, 2, 8, 128), f32),
            pltpu.VMEM((2, N_DEV, 2, 8, 128), f32),
            pltpu.VMEM((2, 2, N_DEV, 8, 128), f32),
            pltpu.VMEM((2, 2, N_DEV, 8, 128), f32),
            pltpu.VMEM((2, 256, 256), jnp.bfloat16),
            pltpu.VMEM((2, 4, 8, 128), f32),
            pltpu.SemaphoreType.DMA((2,)),
            pltpu.SemaphoreType.DMA((7,)),
            pltpu.SemaphoreType.DMA((7,)),
        ],
        compiler_params=pltpu.CompilerParams(has_side_effects=True),
        name="register",
    )(
        amplitudes.reshape(2, N_DEV, 2, 8, 128),
        energies.reshape(N_DEV, 2, 8, 128),
        diagonal_angles,
        turn_angles,
    )
    return out.reshape(2, 16, 128, 128)


def solution(mesh):
    split = P(None, ("bank", "lane"), None, None)
    in_specs = (split, P(("bank", "lane"), None, None), P(), P())
    return jax.shard_map(body, mesh=mesh, in_specs=in_specs, out_specs=split, check_vma=False)
```

time: 327 us -> 82.3 us (0.25)
  waiting for transfers between devices: 133 us -> 0 us
  blocking collectives: 101 us -> 0 us
  Pallas kernels: 0 us -> 79 us
  starting transfers between devices: 28.4 us -> 0 us
  matrix products: 20 us -> 0 us
  local copies, waits for them, and re-layouts: 20.3 us -> 3.14 us
  other arithmetic: 11.5 us -> 0 us
  between operations: 11.5 us -> 0.01 us
    all_to_all x5 -> x0, waiting for transfers between devices: 133 us -> none  [the longest x2 56 us: body(): lax.all_to_all(values, 'lane', split_axis=3, concat_axis=1, tiled=True)]
    all_to_all x5 -> x0, blocking collectives: 101 us -> none  [the longest x4 69.1 us: moved_by_axis(): filled = lax.all_to_all(filled, axes[k], k, k, tiled=True)]
    pallas_call x0 -> x1, Pallas kernels: none -> 79 us  [body(): pl.pallas_call(kernel, out_shape=jax.ShapeDtypeStruct((2, N_DEV, 2, 8, 12...]
    all_to_all x5 -> x0, starting transfers between devices: 28.4 us -> none  [the longest x2 11.7 us: body(): lax.all_to_all(values, BANK, split_axis=2, concat_axis=1, tiled=True)]
    dot_general x8 -> x0, matrix products: 20 us -> none  [mix_dim(): jnp.tensordot(values, real_part, axes=([dim], [0]), precision=lax.Precisi...]
    another operation x2 -> x0, other arithmetic: 11.3 us -> none  [phase_step(): jnp.stack([values[0] * jnp.cos(turn) + values[1] * jnp.sin(turn), values[...]
    reshape x6 -> x0, local copies, waits for them, and re-layouts: 8.02 us -> none  [the longest x2 3.93 us: in_order(): return jnp.moveaxis(tiles, 0, dim).reshape(lengths)]
    transpose x4 -> x0, local copies, waits for them, and re-layouts: 5.18 us -> none  [mix_dim(): return jnp.moveaxis(moved, -1, dim)]
  transfers between devices with their start and end apart: 5 -> 0, of which waited for: 5 -> 0; matrix products, arithmetic and copies ran while one was open for 0% -> 0% of each run, Pallas kernels for 0% -> 0%
where the time goes in v1:
time: 82.3 us; the launch traced here: 82.1 us
  Pallas kernels  79 us (96%)
  local copies, waits for them, and re-layouts  3.14 us (4%)
    pallas_call x1, Pallas kernels, body(): pl.pallas_call(kernel, out_shape=jax.ShapeDtypeStruct((2, N_DEV, 2, 8, 12...  79 us
    unnamed x1, local copies, waits for them, and re-layouts  3.14 us

profile of v1, /device:TPU:1, one launch (start us, length us, event | category | flops | bytes accessed | tf_op | source)
XLA Modules:
  0.0 82.1 jit_solution(4062838044655782958)
XLA Ops:
  0.0 79.0 %register.1 = f32[2,128,2,8,128]{4,3,2,1,0:T(8,128)} custom-call(f32[2,128,2,8,128]{4,3,2,1,0:T(8,128)} %bitcast.4, f32[128,2,8,128]{3,2,1,0:T(8,128)} %bitcast.5, f32[2,128]{1,0:T(2,128)} %diag.1, f32[2,4]{1,0:T(2,128)} %turn.1), custom_call_target="tpu_custom_call" | custom-call | tf_op jit(solution)/shard_map/register/pallas_call | solution.py:271
  79.0 3.1 %copy.6 = f32[2,16,128,128]{3,2,1,0:T(8,128)} copy(f32[2,16,128,128]{3,2,1,0:T(8,128)} %bitcast.3) | data formatting | bytes 4194304

commit v2 on v1

v2 whole, which is shorter than its diff:
```python
import itertools

import jax
import jax.numpy as jnp
from jax import lax
from jax.experimental import pallas as pl
from jax.experimental.pallas import tpu as pltpu
from jax.sharding import PartitionSpec as P

N_DEV = 128
N_LANE = 16
BITS = 7


def place():
    return lax.axis_index("bank"), lax.axis_index("lane")


def hops(step):
    return min(step, 4 - step)


STEPS = sorted(
    (s for s in itertools.product(range(4), range(2), range(4), range(4)) if any(s)),
    key=lambda s: -hops(s[0]) - hops(s[2]) - hops(s[3]),
)


def others():
    bank, lane = place()
    x, core, z, y = bank // 2, lax.rem(bank, 2), lane // 4, lax.rem(lane, 4)
    xs = [lax.rem(x + s, 4) * 2 for s in range(4)]
    cores = [core, 1 - core]
    zs = [lax.rem(z + s, 4) * 4 for s in range(4)]
    ys = [lax.rem(y + s, 4) for s in range(4)]
    banks = {(i, j): xs[i] + cores[j] for i in range(4) for j in range(2)}
    lanes = {(i, j): zs[i] + ys[j] for i in range(4) for j in range(4)}
    found = []
    for sx, sc, sz, sy in STEPS:
        to_bank, to_lane = banks[sx, sc], lanes[sz, sy]
        found.append(((to_bank, to_lane), to_bank * N_LANE + to_lane))
    return found


def send_all(devices, pick_src, dst, send_sem, recv_sem):
    for device, index in devices:
        pltpu.make_async_remote_copy(
            src_ref=pick_src(index),
            dst_ref=dst,
            send_sem=send_sem,
            recv_sem=recv_sem,
            device_id=device,
            device_id_type=pl.DeviceIdType.MESH,
        ).start()


def wait_bytes(ref, sem):
    pltpu.make_async_copy(ref, ref, sem).wait()


def cos_sin(half):
    sq = half * half
    s = 1.0 / 6227020800.0
    for term in (-1.0 / 39916800.0, 1.0 / 362880.0, -1.0 / 5040.0, 1.0 / 120.0, -1.0 / 6.0):
        s = s * sq + term
    s = half + half * (sq * s)
    c = 1.0 / 479001600.0
    for term in (-1.0 / 3628800.0, 1.0 / 40320.0, -1.0 / 720.0, 1.0 / 24.0, -0.5):
        c = c * sq + term
    c = 1.0 + sq * c
    twice = s + s
    return 1.0 - twice * s, twice * c


def butterfly(tiles, tan):
    tiles = list(tiles)
    step = 1
    while step < len(tiles):
        for i in range(len(tiles)):
            if i & step:
                continue
            u, v = tiles[i], tiles[i + step]
            tiles[i] = u - tan * v
            tiles[i + step] = v + tan * u
        step *= 2
    return tiles


def rotate_phase(re, im, half):
    c, s = cos_sin(half)
    return re * c + im * s, im * c - re * s


def sublane_mix(values, tan):
    place_in = lax.broadcasted_iota(jnp.int32, values.shape, 1)
    for step in (4, 2, 1):
        upper = (place_in // step) % 2 == 1
        below = pltpu.roll(values, step, 1)
        other = below if step == 4 else jnp.where(upper, below, pltpu.roll(values, 8 - step, 1))
        values = values + jnp.where(upper, tan, -tan) * other
    return values


def lane_table(cos, sin, scale):
    row = lax.broadcasted_iota(jnp.int32, (128, 128), 0)
    col = lax.broadcasted_iota(jnp.int32, (128, 128), 1)
    table = jnp.broadcast_to(scale, (128, 128))
    for bit in range(BITS):
        r = (row // 2**bit) % 2
        c = (col // 2**bit) % 2
        table = table * jnp.where(r == c, cos, jnp.where(r > c, -sin, sin))
    high = table.astype(jnp.bfloat16)
    low = (table - high.astype(jnp.float32)).astype(jnp.bfloat16)
    both = jnp.concatenate([high, low], axis=1)
    return jnp.concatenate([both, both], axis=0)


def lane_mix(values, table):
    high = values.astype(jnp.bfloat16)
    low = (values - high.astype(jnp.float32)).astype(jnp.bfloat16)
    parts = jnp.concatenate([high, low], axis=1)
    out = jnp.dot(parts, table, preferred_element_type=jnp.float32)
    return out[:, :128] + out[:, 128:]


def kernel(amp, energy, diag_any, turn_any, out, diag, turn, a_in, fwd, mid, back, fin, tables, tans, sems, sends, recvs):
    bank, lane = place()
    me = bank * N_LANE + lane
    scope = jax.named_scope

    gets = [pltpu.make_async_copy(energy.at[:, k], fwd.at[k, :, 2], sems.at[k]) for k in range(2)]
    gets += [pltpu.make_async_copy(amp, a_in, sems.at[2])]
    small = [pltpu.make_async_copy(diag_any, diag, sems.at[3]), pltpu.make_async_copy(turn_any, turn, sems.at[4])]
    for get in small + gets:
        get.start()

    devices = others()
    barrier = pltpu.get_barrier_semaphore()
    with scope("signals"):
        for device, _ in devices:
            pl.semaphore_signal(barrier, 1, device_id=device, device_id_type=pl.DeviceIdType.MESH)

    with scope("tables"):
        for get in small:
            get.wait()
        cos, sin = cos_sin(turn[...] * 0.5)
        tan = sin / cos
        for layer in range(2):
            for group in range(4):
                tans[layer, group] = jnp.broadcast_to(tan[layer : layer + 1, group : group + 1], (8, 128))
            c = [cos[layer : layer + 1, g : g + 1] for g in range(4)]
            c12 = c[1] * c[2]
            c12_2 = c12 * c12
            c3_2 = c[3] * c[3]
            scale = c12_2 * c12_2 * c12_2 * c12 * c3_2 * c3_2
            tables[layer] = lane_table(c[0], sin[layer : layer + 1, 0:1], scale)

    with scope("wait_in"):
        for get in gets:
            get.wait()

    def first(i, carry):
        at = pl.ds(i * 8, 8)
        angle = (diag[0:1, :] * 0.5).reshape(1, 1, 1, 128)
        half = jnp.stack([fwd[0, at, 2], fwd[1, at, 2]], axis=1) * angle
        re, im = rotate_phase(a_in[0, at], a_in[1, at], half)
        values = jnp.concatenate([re, im], axis=0)
        mixed = lane_mix(values.reshape(256, 128), tables[0]).reshape(32, 8, 128)
        mixed = sublane_mix(mixed, tans[0, 1, 0:1, :].reshape(1, 1, 128))
        mixed = mixed.reshape(2, 16, 8, 128)
        tan1 = tans[0, 1]
        for part in range(2):
            tiles = butterfly([mixed[part, j] for j in range(16)], tan1)
            for j in range(16):
                a_in[part, i * 8 + j // 2, j % 2] = tiles[j]
        return carry

    with scope("first"):
        lax.fori_loop(0, 16, first, 0)

    tan2 = tans[0, 2]
    for k in range(2):

        def blocks(i, carry):
            part, row = i // 8, lax.rem(i, 8)
            tiles = butterfly([a_in[part, b * 8 + row, k] for b in range(16)], tan2)
            for b in range(16):
                fwd[k, b * 8 + row, part] = tiles[b]
            return carry

        with scope(f"blocks_{k}"):
            lax.fori_loop(0, 16, blocks, 0)
        if k == 0:
            with scope("barrier"):
                pl.semaphore_wait(barrier, N_DEV - 1)
        with scope(f"send_f{k}"):
            send_all(devices, lambda i: fwd.at[k, i], mid.at[k, me], sends.at[k], recvs.at[k])
        mid[k, me] = fwd[k, me]

    for k in range(2):
        with scope(f"wait_m{k}"):
            wait_bytes(mid.at[k, pl.ds(0, N_DEV - 1)], recvs.at[k])

        def lanes_1(i, carry):
            b, part = i // 2, lax.rem(i, 2)
            tiles = butterfly([mid[k, b * 16 + l, part] for l in range(16)], tans[0, 3])
            for l in range(16):
                mid[k, b * 16 + l, part] = tiles[l]
            return carry

        def banks(l, carry):
            re = butterfly([mid[k, b * 16 + l, 0] for b in range(8)], tans[0, 2])
            im = butterfly([mid[k, b * 16 + l, 1] for b in range(8)], tans[0, 2])
            angle = diag[1:2, :] * 0.5
            for b in range(8):
                re[b], im[b] = rotate_phase(re[b], im[b], mid[k, b * 16 + l, 2] * angle)
            re = butterfly(re, tans[1, 2])
            im = butterfly(im, tans[1, 2])
            for b in range(8):
                mid[k, b * 16 + l, 0] = re[b]
                mid[k, b * 16 + l, 1] = im[b]
            return carry

        def lanes_2(b, carry):
            both = []
            for part in range(2):
                tiles = butterfly([mid[k, b * 16 + l, part] for l in range(16)], tans[1, 3])
                both.append(jnp.stack(tiles))
            values = jnp.stack(both).reshape(256, 128)
            mixed = lane_mix(values, tables[1]).reshape(32, 8, 128)
            mixed = sublane_mix(mixed, tans[1, 1, 0:1, :].reshape(1, 1, 128))
            mixed = mixed.reshape(2, 16, 8, 128)
            for part in range(2):
                back[k, pl.ds(b * 16, 16), part] = mixed[part]
            return carry

        with scope(f"mid_{k}"):
            lax.fori_loop(0, 16, lanes_1, 0)
            lax.fori_loop(0, 16, banks, 0)
            lax.fori_loop(0, 8, lanes_2, 0)
        with scope(f"send_b{k}"):
            if k == 0:
                send_all(devices, lambda i: back.at[0, i], fin.at[0, me], sends.at[2], recvs.at[2])
            else:
                for part in range(2):
                    n = 3 + part
                    send_all(
                        devices, lambda i: back.at[1, i, part], fin.at[1, me, part], sends.at[n], recvs.at[n]
                    )
        fin[k, me] = back[k, me]

    for k in range(2):
        for part in range(2):
            with scope(f"wait_b{k}{part}"):
                if k == 1:
                    wait_bytes(fin.at[1, pl.ds(0, N_DEV - 1), part], recvs.at[3 + part])
                elif part == 0:
                    wait_bytes(fin.at[0, pl.ds(0, N_DEV - 1)], recvs.at[2])

            def rows(b, carry):
                tiles = butterfly([fin[k, b * 8 + r, part] for r in range(8)], tans[1, 1])
                for r in range(8):
                    fin[k, b * 8 + r, part] = tiles[r]
                return carry

            def last(r, carry):
                tiles = butterfly([fin[k, b * 8 + r, part] for b in range(16)], tans[1, 2])
                if k == 0:
                    for b in range(16):
                        fin[0, b * 8 + r, part] = tiles[b]
                else:
                    t = tans[1, 1]
                    for b in range(16):
                        u = fin[0, b * 8 + r, part]
                        v = tiles[b]
                        out[part, b * 8 + r, 0] = u - t * v
                        out[part, b * 8 + r, 1] = v + t * u
                return carry

            with scope(f"last_{k}{part}"):
                lax.fori_loop(0, 16, rows, 0)
                lax.fori_loop(0, 8, last, 0)

    for k in range(2):
        wait_bytes(fwd.at[k, pl.ds(0, N_DEV - 1)], sends.at[k])
    wait_bytes(back.at[0, pl.ds(0, N_DEV - 1)], sends.at[2])
    for part in range(2):
        wait_bytes(back.at[1, pl.ds(0, N_DEV - 1), part], sends.at[3 + part])


def body(amplitudes, energies, diagonal_angles, turn_angles):
    f32 = jnp.float32
    anywhere = pl.BlockSpec(memory_space=pl.ANY)
    vmem = pl.BlockSpec(memory_space=pltpu.VMEM)
    out = pl.pallas_call(
        kernel,
        out_shape=pltpu.VMEM((2, N_DEV, 2, 8, 128), f32),
        in_specs=[anywhere] * 4,
        out_specs=vmem,
        scratch_shapes=[
            pltpu.VMEM((2, 128), f32),
            pltpu.VMEM((2, 4), f32),
            pltpu.VMEM((2, N_DEV, 2, 8, 128), f32),
            pltpu.VMEM((2, N_DEV, 3, 8, 128), f32),
            pltpu.VMEM((2, N_DEV, 3, 8, 128), f32),
            pltpu.VMEM((2, N_DEV, 2, 8, 128), f32),
            pltpu.VMEM((2, N_DEV, 2, 8, 128), f32),
            pltpu.VMEM((2, 256, 256), jnp.bfloat16),
            pltpu.VMEM((2, 4, 8, 128), f32),
            pltpu.SemaphoreType.DMA((5,)),
            pltpu.SemaphoreType.DMA((5,)),
            pltpu.SemaphoreType.DMA((5,)),
        ],
        compiler_params=pltpu.CompilerParams(
            collective_id=0, has_side_effects=True, vmem_limit_bytes=24 * 1024 * 1024
        ),
        name="register",
    )(
        *(
            pltpu.with_memory_space_constraint(array, pltpu.HBM)
            for array in (
                amplitudes.reshape(2, N_DEV, 2, 8, 128),
                energies.reshape(N_DEV, 2, 8, 128),
                diagonal_angles,
                turn_angles,
            )
        )
    )
    return out.reshape(2, 16, 128, 128)


def solution(mesh):
    split = P(None, ("bank", "lane"), None, None)
    in_specs = (split, P(("bank", "lane"), None, None), P(), P())
    return jax.shard_map(body, mesh=mesh, in_specs=in_specs, out_specs=split, check_vma=False)
```

time: 82.3 us -> 74.7 us (0.908)
  Pallas kernels: 79 us -> 73.2 us
  local copies, waits for them, and re-layouts: 3.14 us -> 1.32 us
    pallas_call x1, Pallas kernels: 79 us -> 73.2 us  [body(): pl.pallas_call(kernel, out_shape=pltpu.VMEM((2, N_DEV, 2, 8, 128), f32),...]
    unnamed x1, local copies, waits for them, and re-layouts: 3.14 us -> 1.32 us
where the time goes in v2:
time: 74.7 us; the launch traced here: 74.6 us
  Pallas kernels  73.2 us (98%)
  local copies, waits for them, and re-layouts  1.32 us (2%)
    pallas_call x1, Pallas kernels, body(): pl.pallas_call(kernel, out_shape=pltpu.VMEM((2, N_DEV, 2, 8, 128), f32),...  73.2 us

profile of v2, /device:TPU:1, one launch (start us, length us, event | category | flops | bytes accessed | tf_op | source)
XLA Modules:
  0.0 74.6 jit_solution(6871544560315713408)
XLA Ops:
  0.0 73.2 %register.1 = f32[2,128,2,8,128]{4,3,2,1,0:T(8,128)S(1)} custom-call(f32[2,128,2,8,128]{4,3,2,1,0:T(8,128)} %bitcast.4, f32[128,2,8,128]{3,2,1,0:T(8,128)} %bitcast.5, f32[2,128]{1,0:T(2,128)} %diag_any.1, f32[2,4]{1,0:T(2,128)} %turn_any.1), custom_call_target="tpu_custom_call" | custom-call | tf_op jit(solution)/shard_map/register/pallas_call | solution.py:295
  73.2 1.3 %copy.6 = f32[2,16,128,128]{3,2,1,0:T(8,128)} copy(f32[2,16,128,128]{3,2,1,0:T(8,128)S(1)} %bitcast.3) | data formatting | bytes 4194304

commit v3 on v2

--- a/solution.py
+++ b/solution.py
@@ -123,15 +123,15 @@
     return out[:, :128] + out[:, 128:]
 
 
-def kernel(amp, energy, diag_any, turn_any, out, diag, turn, a_in, fwd, mid, back, fin, tables, tans, sems, sends, recvs):
+def kernel(amp, energy, diag_any, turn_any, out, diag, turn, a_in, e_in, e_rx, fwd, mid, back, fin, tables, tans, sems, sends, recvs):
     bank, lane = place()
     me = bank * N_LANE + lane
     scope = jax.named_scope
 
-    gets = [pltpu.make_async_copy(energy.at[:, k], fwd.at[k, :, 2], sems.at[k]) for k in range(2)]
-    gets += [pltpu.make_async_copy(amp, a_in, sems.at[2])]
-    small = [pltpu.make_async_copy(diag_any, diag, sems.at[3]), pltpu.make_async_copy(turn_any, turn, sems.at[4])]
-    for get in small + gets:
+    get_e = pltpu.make_async_copy(energy, e_in, sems.at[0])
+    get_a = pltpu.make_async_copy(amp, a_in, sems.at[1])
+    small = [pltpu.make_async_copy(diag_any, diag, sems.at[2]), pltpu.make_async_copy(turn_any, turn, sems.at[3])]
+    for get in [get_e, *small, get_a]:
         get.start()
 
     devices = others()
@@ -156,13 +156,18 @@
             tables[layer] = lane_table(c[0], sin[layer : layer + 1, 0:1], scale)
 
     with scope("wait_in"):
-        for get in gets:
-            get.wait()
+        get_e.wait()
+        get_a.wait()
+    with scope("barrier"):
+        pl.semaphore_wait(barrier, N_DEV - 1)
+    with scope("send_e"):
+        send_all(devices, lambda i: e_in.at[i], e_rx.at[me], sends.at[5], recvs.at[5])
+    e_rx[me] = e_in[me]
 
     def first(i, carry):
         at = pl.ds(i * 8, 8)
         angle = (diag[0:1, :] * 0.5).reshape(1, 1, 1, 128)
-        half = jnp.stack([fwd[0, at, 2], fwd[1, at, 2]], axis=1) * angle
+        half = e_in[at] * angle
         re, im = rotate_phase(a_in[0, at], a_in[1, at], half)
         values = jnp.concatenate([re, im], axis=0)
         mixed = lane_mix(values.reshape(256, 128), tables[0]).reshape(32, 8, 128)
@@ -190,13 +195,12 @@
 
         with scope(f"blocks_{k}"):
             lax.fori_loop(0, 16, blocks, 0)
-        if k == 0:
-            with scope("barrier"):
-                pl.semaphore_wait(barrier, N_DEV - 1)
         with scope(f"send_f{k}"):
             send_all(devices, lambda i: fwd.at[k, i], mid.at[k, me], sends.at[k], recvs.at[k])
         mid[k, me] = fwd[k, me]
 
+    with scope("wait_e"):
+        wait_bytes(e_rx.at[pl.ds(0, N_DEV - 1)], recvs.at[5])
     for k in range(2):
         with scope(f"wait_m{k}"):
             wait_bytes(mid.at[k, pl.ds(0, N_DEV - 1)], recvs.at[k])
@@ -213,7 +217,7 @@
             im = butterfly([mid[k, b * 16 + l, 1] for b in range(8)], tans[0, 2])
             angle = diag[1:2, :] * 0.5
             for b in range(8):
-                re[b], im[b] = rotate_phase(re[b], im[b], mid[k, b * 16 + l, 2] * angle)
+                re[b], im[b] = rotate_phase(re[b], im[b], e_rx[b * 16 + l, k] * angle)
             re = butterfly(re, tans[1, 2])
             im = butterfly(im, tans[1, 2])
             for b in range(8):
@@ -281,6 +285,7 @@
                 lax.fori_loop(0, 16, rows, 0)
                 lax.fori_loop(0, 8, last, 0)
 
+    wait_bytes(e_in.at[pl.ds(0, N_DEV - 1)], sends.at[5])
     for k in range(2):
         wait_bytes(fwd.at[k, pl.ds(0, N_DEV - 1)], sends.at[k])
     wait_bytes(back.at[0, pl.ds(0, N_DEV - 1)], sends.at[2])
@@ -301,15 +306,17 @@
             pltpu.VMEM((2, 128), f32),
             pltpu.VMEM((2, 4), f32),
             pltpu.VMEM((2, N_DEV, 2, 8, 128), f32),
-            pltpu.VMEM((2, N_DEV, 3, 8, 128), f32),
-            pltpu.VMEM((2, N_DEV, 3, 8, 128), f32),
+            pltpu.VMEM((N_DEV, 2, 8, 128), f32),
+            pltpu.VMEM((N_DEV, 2, 8, 128), f32),
+            pltpu.VMEM((2, N_DEV, 2, 8, 128), f32),
+            pltpu.VMEM((2, N_DEV, 2, 8, 128), f32),
             pltpu.VMEM((2, N_DEV, 2, 8, 128), f32),
             pltpu.VMEM((2, N_DEV, 2, 8, 128), f32),
             pltpu.VMEM((2, 256, 256), jnp.bfloat16),
             pltpu.VMEM((2, 4, 8, 128), f32),
-            pltpu.SemaphoreType.DMA((5,)),
-            pltpu.SemaphoreType.DMA((5,)),
-            pltpu.SemaphoreType.DMA((5,)),
+            pltpu.SemaphoreType.DMA((4,)),
+            pltpu.SemaphoreType.DMA((6,)),
+            pltpu.SemaphoreType.DMA((6,)),
         ],
         compiler_params=pltpu.CompilerParams(
             collective_id=0, has_side_effects=True, vmem_limit_bytes=24 * 1024 * 1024

time: 74.7 us -> 71.1 us (0.952)
  Pallas kernels: 73.2 us -> 69.6 us
    pallas_call x1, Pallas kernels: 73.2 us -> 69.6 us  [body(): pl.pallas_call(kernel, out_shape=pltpu.VMEM((2, N_DEV, 2, 8, 128), f32),...]
where the time goes in v3:
time: 71.1 us; the launch traced here: 70.9 us
  Pallas kernels  69.6 us (98%)
  local copies, waits for them, and re-layouts  1.32 us (2%)
    pallas_call x1, Pallas kernels, body(): pl.pallas_call(kernel, out_shape=pltpu.VMEM((2, N_DEV, 2, 8, 128), f32),...  69.6 us

profile of v3, /device:TPU:1, one launch (start us, length us, event | category | flops | bytes accessed | tf_op | source)
XLA Modules:
  0.0 70.9 jit_solution(11517595441746379137)
XLA Ops:
  0.0 69.6 %register.1 = f32[2,128,2,8,128]{4,3,2,1,0:T(8,128)S(1)} custom-call(f32[2,128,2,8,128]{4,3,2,1,0:T(8,128)} %bitcast.4, f32[128,2,8,128]{3,2,1,0:T(8,128)} %bitcast.5, f32[2,128]{1,0:T(2,128)} %diag_any.1, f32[2,4]{1,0:T(2,128)} %turn_any.1), custom_call_target="tpu_custom_call" | custom-call | tf_op jit(solution)/shard_map/register/pallas_call | solution.py:300
  69.6 1.3 %copy.6 = f32[2,16,128,128]{3,2,1,0:T(8,128)} copy(f32[2,16,128,128]{3,2,1,0:T(8,128)S(1)} %bitcast.3) | data formatting | bytes 4194304

commit v4 on v3

--- a/solution.py
+++ b/solution.py
@@ -26,7 +26,27 @@
 )
 
 
-def others():
+MIXED = sorted(STEPS, key=lambda s: (s[0] * 29 + s[1] * 53 + s[2] * 17 + s[3] * 71) * 37 % 127)
+
+
+def lines(step):
+    return int(any(step[:2])) + int(step[2] > 0) + int(step[3] > 0)
+
+
+def along(step, line):
+    part = [(step[0], step[1], 0, 0), (0, 0, step[2], 0), (0, 0, 0, step[3])]
+    rest = [(0, 0, step[2], step[3]), (step[0], step[1], 0, step[3]), (step[0], step[1], step[2], 0)]
+    return part[line], rest[line]
+
+
+def reverse(step):
+    return ((4 - step[0]) % 4, step[1], (4 - step[2]) % 4, (4 - step[3]) % 4)
+
+
+RELAYED = [(s, (s[0] * 2 + s[1] + s[2] + s[3]) % 3) for s in MIXED if lines(s) == 3]
+
+
+def spots():
     bank, lane = place()
     x, core, z, y = bank // 2, lax.rem(bank, 2), lane // 4, lax.rem(lane, 4)
     xs = [lax.rem(x + s, 4) * 2 for s in range(4)]
@@ -35,23 +55,28 @@
     ys = [lax.rem(y + s, 4) for s in range(4)]
     banks = {(i, j): xs[i] + cores[j] for i in range(4) for j in range(2)}
     lanes = {(i, j): zs[i] + ys[j] for i in range(4) for j in range(4)}
-    found = []
-    for sx, sc, sz, sy in STEPS:
-        to_bank, to_lane = banks[sx, sc], lanes[sz, sy]
-        found.append(((to_bank, to_lane), to_bank * N_LANE + to_lane))
-    return found
+
+    def spot(step):
+        to_bank, to_lane = banks[step[:2]], lanes[step[2:]]
+        return (to_bank, to_lane), to_bank * N_LANE + to_lane
+
+    return spot
+
+
+def send(src, dst, device, send_sem, recv_sem):
+    pltpu.make_async_remote_copy(
+        src_ref=src,
+        dst_ref=dst,
+        send_sem=send_sem,
+        recv_sem=recv_sem,
+        device_id=device,
+        device_id_type=pl.DeviceIdType.MESH,
+    ).start()
 
 
 def send_all(devices, pick_src, dst, send_sem, recv_sem):
     for device, index in devices:
-        pltpu.make_async_remote_copy(
-            src_ref=pick_src(index),
-            dst_ref=dst,
-            send_sem=send_sem,
-            recv_sem=recv_sem,
-            device_id=device,
-            device_id_type=pl.DeviceIdType.MESH,
-        ).start()
+        send(pick_src(index), dst, device, send_sem, recv_sem)
 
 
 def wait_bytes(ref, sem):
@@ -123,10 +148,43 @@
     return out[:, :128] + out[:, 128:]
 
 
-def kernel(amp, energy, diag_any, turn_any, out, diag, turn, a_in, e_in, e_rx, fwd, mid, back, fin, tables, tans, sems, sends, recvs):
+def home_rows(src, dst, tan):
+    def one(b, carry):
+        tiles = butterfly([src[b * 8 + r] for r in range(8)], tan[0])
+        for r in range(8):
+            dst[b * 8 + r] = tiles[r]
+        return carry
+
+    lax.fori_loop(0, 16, one, 0)
+
+
+def home_blocks(pick, pick_other, dst, r, tan):
+    tiles = butterfly([pick(b * 8 + r) for b in range(16)], tan[1])
+    for b in range(16):
+        u, v = pick_other(b * 8 + r), tiles[b]
+        dst[b, r, 0] = u - tan[0] * v
+        dst[b, r, 1] = v + tan[0] * u
+
+
+def finish(done, half_done, raw, tan, out, rows, stage, sems):
+    copies = [pltpu.make_async_copy(done.at[pl.ds(i * 4, 4)], out.at[0, pl.ds(i * 4, 4)], sems.at[i]) for i in range(4)]
+    for copy in copies:
+        copy.start()
+    home_rows(raw, rows, tan)
+    for r in range(8):
+        home_blocks(lambda d: rows[d], lambda d: half_done[d], stage, r, tan)
+        if r % 2:
+            copies.append(pltpu.make_async_copy(stage.at[:, pl.ds(r - 1, 2)], out.at[1, :, pl.ds(r - 1, 2)], sems.at[4 + r // 2]))
+            copies[-1].start()
+    for copy in copies:
+        copy.wait()
+
+
+def kernel(amp, energy, diag_any, turn_any, done, half_done, raw, tan_out, diag, turn, a_in, e_in, e_rx, relay, fwd, mid, back, fin, fin_1, tables, tans, sems, sends, recvs, met):
     bank, lane = place()
     me = bank * N_LANE + lane
     scope = jax.named_scope
+    late = [fin_1, raw]
 
     get_e = pltpu.make_async_copy(energy, e_in, sems.at[0])
     get_a = pltpu.make_async_copy(amp, a_in, sems.at[1])
@@ -134,14 +192,39 @@
     for get in [get_e, *small, get_a]:
         get.start()
 
-    devices = others()
-    barrier = pltpu.get_barrier_semaphore()
-    with scope("signals"):
-        for device, _ in devices:
-            pl.semaphore_signal(barrier, 1, device_id=device, device_id_type=pl.DeviceIdType.MESH)
+    spot = spots()
+    devices = [spot(step) for step in STEPS]
+    mixed = [spot(step) for step in MIXED]
+    near = [spot(step)[0] for step in MIXED if lines(step) == 1]
+    rounds = [pltpu.get_barrier_semaphore(), met.at[0], met.at[1]]
+
+    def signal(n):
+        for device in near:
+            pl.semaphore_signal(rounds[n], 1, device_id=device, device_id_type=pl.DeviceIdType.MESH)
+
+    def meet(n):
+        with scope(f"meet_{n}"):
+            pl.semaphore_wait(rounds[n], len(near))
+        if n < 2:
+            signal(n + 1)
+
+    def send_e(n):
+        some = [spot(step) for step in MIXED if lines(step) == n]
+        send_all(some, lambda i: e_in.at[i], e_rx.at[me], sends.at[5], recvs.at[5])
+
+    signal(0)
+    with scope("wait_in"):
+        get_e.wait()
+    meet(0)
+    with scope("send_e0"):
+        send_e(1)
+        for j, (step, line) in enumerate(RELAYED):
+            device, _ = spot(along(step, line)[0])
+            send(e_in.at[spot(step)[1]], relay.at[j], device, sends.at[5], recvs.at[6])
+    e_rx[me] = e_in[me]
 
     with scope("tables"):
-        for get in small:
+        for get in [*small, get_a]:
             get.wait()
         cos, sin = cos_sin(turn[...] * 0.5)
         tan = sin / cos
@@ -154,15 +237,6 @@
             c3_2 = c[3] * c[3]
             scale = c12_2 * c12_2 * c12_2 * c12 * c3_2 * c3_2
             tables[layer] = lane_table(c[0], sin[layer : layer + 1, 0:1], scale)
-
-    with scope("wait_in"):
-        get_e.wait()
-        get_a.wait()
-    with scope("barrier"):
-        pl.semaphore_wait(barrier, N_DEV - 1)
-    with scope("send_e"):
-        send_all(devices, lambda i: e_in.at[i], e_rx.at[me], sends.at[5], recvs.at[5])
-    e_rx[me] = e_in[me]
 
     def first(i, carry):
         at = pl.ds(i * 8, 8)
@@ -180,8 +254,21 @@
                 a_in[part, i * 8 + j // 2, j % 2] = tiles[j]
         return carry
 
-    with scope("first"):
-        lax.fori_loop(0, 16, first, 0)
+    with scope("first_0"):
+        lax.fori_loop(0, 4, first, 0)
+    meet(1)
+    send_e(2)
+    with scope("first_1"):
+        lax.fori_loop(4, 8, first, 0)
+    with scope("wait_r"):
+        wait_bytes(relay, recvs.at[6])
+    with scope("relay"):
+        for j, (step, line) in enumerate(RELAYED):
+            part, rest = along(step, line)
+            send(relay.at[j], e_rx.at[spot(reverse(part))[1]], spot(rest)[0], sends.at[6], recvs.at[5])
+    with scope("first_2"):
+        lax.fori_loop(8, 16, first, 0)
+    meet(2)
 
     tan2 = tans[0, 2]
     for k in range(2):
@@ -196,7 +283,7 @@
         with scope(f"blocks_{k}"):
             lax.fori_loop(0, 16, blocks, 0)
         with scope(f"send_f{k}"):
-            send_all(devices, lambda i: fwd.at[k, i], mid.at[k, me], sends.at[k], recvs.at[k])
+            send_all(mixed, lambda i: fwd.at[k, i], mid.at[k, me], sends.at[k], recvs.at[k])
         mid[k, me] = fwd[k, me]
 
     with scope("wait_e"):
@@ -244,48 +331,52 @@
             lax.fori_loop(0, 8, lanes_2, 0)
         with scope(f"send_b{k}"):
             if k == 0:
-                send_all(devices, lambda i: back.at[0, i], fin.at[0, me], sends.at[2], recvs.at[2])
+                send_all(mixed, lambda i: back.at[0, i], fin.at[me], sends.at[2], recvs.at[2])
             else:
                 for part in range(2):
                     n = 3 + part
                     send_all(
-                        devices, lambda i: back.at[1, i, part], fin.at[1, me, part], sends.at[n], recvs.at[n]
+                        devices, lambda i: back.at[1, i, part], late[part].at[me], sends.at[n], recvs.at[n]
                     )
-        fin[k, me] = back[k, me]
-
-    for k in range(2):
+        if k == 0:
+            fin[me] = back[0, me]
+        else:
+            for part in range(2):
+                late[part][me] = back[1, me, part]
+
+    with scope("wait_b0"):
+        wait_bytes(fin.at[pl.ds(0, N_DEV - 1)], recvs.at[2])
+    tan_out[0] = tans[1, 1]
+    tan_out[1] = tans[1, 2]
+    with scope("last_0"):
         for part in range(2):
-            with scope(f"wait_b{k}{part}"):
-                if k == 1:
-                    wait_bytes(fin.at[1, pl.ds(0, N_DEV - 1), part], recvs.at[3 + part])
-                elif part == 0:
-                    wait_bytes(fin.at[0, pl.ds(0, N_DEV - 1)], recvs.at[2])
-
-            def rows(b, carry):
-                tiles = butterfly([fin[k, b * 8 + r, part] for r in range(8)], tans[1, 1])
-                for r in range(8):
-                    fin[k, b * 8 + r, part] = tiles[r]
+            home_rows(fin.at[:, part], fin.at[:, part], tan_out)
+
+            def last(r, carry):
+                tiles = butterfly([fin[b * 8 + r, part] for b in range(16)], tan_out[1])
+                for b in range(16):
+                    if part == 0:
+                        fin[b * 8 + r, 0] = tiles[b]
+                    else:
+                        half_done[b * 8 + r] = tiles[b]
                 return carry
 
-            def last(r, carry):
-                tiles = butterfly([fin[k, b * 8 + r, part] for b in range(16)], tans[1, 2])
-                if k == 0:
-                    for b in range(16):
-                        fin[0, b * 8 + r, part] = tiles[b]
-                else:
-                    t = tans[1, 1]
-                    for b in range(16):
-                        u = fin[0, b * 8 + r, part]
-                        v = tiles[b]
-                        out[part, b * 8 + r, 0] = u - t * v
-                        out[part, b * 8 + r, 1] = v + t * u
-                return carry
-
-            with scope(f"last_{k}{part}"):
-                lax.fori_loop(0, 16, rows, 0)
-                lax.fori_loop(0, 8, last, 0)
+            lax.fori_loop(0, 8, last, 0)
+    with scope("wait_b10"):
+        wait_bytes(fin_1.at[pl.ds(0, N_DEV - 1)], recvs.at[3])
+    with scope("last_10"):
+        home_rows(fin_1, fin_1, tan_out)
+
+        def last_0(r, carry):
+            home_blocks(lambda d: fin_1[d], lambda d: fin[d, 0], done, r, tan_out)
+            return carry
+
+        lax.fori_loop(0, 8, last_0, 0)
+    with scope("wait_b11"):
+        wait_bytes(raw.at[pl.ds(0, N_DEV - 1)], recvs.at[4])
 
     wait_bytes(e_in.at[pl.ds(0, N_DEV - 1)], sends.at[5])
+    wait_bytes(relay, sends.at[6])
     for k in range(2):
         wait_bytes(fwd.at[k, pl.ds(0, N_DEV - 1)], sends.at[k])
     wait_bytes(back.at[0, pl.ds(0, N_DEV - 1)], sends.at[2])
@@ -297,26 +388,34 @@
     f32 = jnp.float32
     anywhere = pl.BlockSpec(memory_space=pl.ANY)
     vmem = pl.BlockSpec(memory_space=pltpu.VMEM)
-    out = pl.pallas_call(
+    done, half_done, raw, tan = pl.pallas_call(
         kernel,
-        out_shape=pltpu.VMEM((2, N_DEV, 2, 8, 128), f32),
+        out_shape=(
+            pltpu.VMEM((16, 8, 2, 8, 128), f32),
+            pltpu.VMEM((N_DEV, 8, 128), f32),
+            pltpu.VMEM((N_DEV, 8, 128), f32),
+            pltpu.VMEM((2, 8, 128), f32),
+        ),
         in_specs=[anywhere] * 4,
-        out_specs=vmem,
+        out_specs=(vmem,) * 4,
         scratch_shapes=[
             pltpu.VMEM((2, 128), f32),
             pltpu.VMEM((2, 4), f32),
             pltpu.VMEM((2, N_DEV, 2, 8, 128), f32),
             pltpu.VMEM((N_DEV, 2, 8, 128), f32),
             pltpu.VMEM((N_DEV, 2, 8, 128), f32),
+            pltpu.VMEM((len(RELAYED), 2, 8, 128), f32),
             pltpu.VMEM((2, N_DEV, 2, 8, 128), f32),
             pltpu.VMEM((2, N_DEV, 2, 8, 128), f32),
             pltpu.VMEM((2, N_DEV, 2, 8, 128), f32),
-            pltpu.VMEM((2, N_DEV, 2, 8, 128), f32),
+            pltpu.VMEM((N_DEV, 2, 8, 128), f32),
+            pltpu.VMEM((N_DEV, 8, 128), f32),
             pltpu.VMEM((2, 256, 256), jnp.bfloat16),
             pltpu.VMEM((2, 4, 8, 128), f32),
             pltpu.SemaphoreType.DMA((4,)),
-            pltpu.SemaphoreType.DMA((6,)),
-            pltpu.SemaphoreType.DMA((6,)),
+            pltpu.SemaphoreType.DMA((7,)),
+            pltpu.SemaphoreType.DMA((7,)),
+            pltpu.SemaphoreType.REGULAR((2,)),
         ],
         compiler_params=pltpu.CompilerParams(
             collective_id=0, has_side_effects=True, vmem_limit_bytes=24 * 1024 * 1024
@@ -333,6 +432,19 @@
             )
         )
     )
+    out = pl.pallas_call(
+        finish,
+        out_shape=jax.ShapeDtypeStruct((2, 16, 8, 2, 8, 128), f32),
+        in_specs=[vmem] * 4,
+        out_specs=anywhere,
+        scratch_shapes=[
+            pltpu.VMEM((N_DEV, 8, 128), f32),
+            pltpu.VMEM((16, 8, 2, 8, 128), f32),
+            pltpu.SemaphoreType.DMA((8,)),
+        ],
+        compiler_params=pltpu.CompilerParams(vmem_limit_bytes=8 * 1024 * 1024),
+        name="finish",
+    )(done, half_done, raw, tan)
     return out.reshape(2, 16, 128, 128)
 
 

time: 71.1 us -> 69.7 us (0.980)
  local copies, waits for them, and re-layouts: 1.32 us -> 0 us
    unnamed x1 -> x0, local copies, waits for them, and re-layouts: 1.32 us -> none
    pallas_call x1 -> x2, Pallas kernels: 69.6 us -> 69.6 us  [the longest x1 68.2 us: body(): pl.pallas_call(kernel, out_shape=(pltpu.VMEM((16, 8, 2, 8, 128), f32), pl...]
where the time goes in v4:
time: 69.7 us; the launch traced here: 69.6 us
  Pallas kernels  69.6 us (100%)
    pallas_call x1, Pallas kernels, body(): pl.pallas_call(kernel, out_shape=(pltpu.VMEM((16, 8, 2, 8, 128), f32), pl...  68.2 us

profile of v4, /device:TPU:1, one launch (start us, length us, event | category | flops | bytes accessed | tf_op | source)
XLA Modules:
  0.0 69.6 jit_solution(13640709505337525467)
XLA Ops:
  0.0 68.2 %register.1 = (f32[16,8,2,8,128]{4,3,2,1,0:T(8,128)S(1)}, f32[128,8,128]{2,1,0:T(8,128)S(1)}, f32[128,8,128]{2,1,0:T(8,128)S(1)}, f32[2,8,128]{2,1,0:T(8,128)S(1)}) custom-call(f32[2,128,2,8,128]{4,3,2,1,0:T(8,128)} %bitcast.3, f32[128,2,8,128]{3,2,1,0:T(8,128)} %bitcast.4, f32[2,128]{1,0:T(2,128)} %diag_any.1, f32[2,4]{1,0:T(2,128)} %turn_any.1), custom_call_target="tpu_custom_call" | custom-call | tf_op jit(solution)/shard_map/register/pallas_call | solution.py:391
  68.2 1.4 %finish.1 = f32[2,16,8,2,8,128]{5,4,3,2,1,0:T(8,128)} custom-call(f32[16,8,2,8,128]{4,3,2,1,0:T(8,128)S(1)} %get-tuple-element.9.done, f32[128,8,128]{2,1,0:T(8,128)S(1)} %get-tuple-element.10.half_done, f32[128,8,128]{2,1,0:T(8,128)S(1)} %get-tuple-element.11.raw, f32[2,8,128]{2,1,0:T(8,128)S(1)} %get-tuple-element.12.tan), custom_call_target="tpu_custom_call" | custom-call | tf_op jit(solution)/shard_map/finish/pallas_call | solution.py:435

commit v5 on v4

--- a/solution.py
+++ b/solution.py
@@ -155,7 +155,7 @@
             dst[b * 8 + r] = tiles[r]
         return carry
 
-    lax.fori_loop(0, 16, one, 0)
+    lax.fori_loop(0, 16, one, 0, unroll=4)
 
 
 def home_blocks(pick, pick_other, dst, r, tan):
@@ -255,11 +255,11 @@
         return carry
 
     with scope("first_0"):
-        lax.fori_loop(0, 4, first, 0)
+        lax.fori_loop(0, 4, first, 0, unroll=2)
     meet(1)
     send_e(2)
     with scope("first_1"):
-        lax.fori_loop(4, 8, first, 0)
+        lax.fori_loop(4, 8, first, 0, unroll=2)
     with scope("wait_r"):
         wait_bytes(relay, recvs.at[6])
     with scope("relay"):
@@ -267,7 +267,7 @@
             part, rest = along(step, line)
             send(relay.at[j], e_rx.at[spot(reverse(part))[1]], spot(rest)[0], sends.at[6], recvs.at[5])
     with scope("first_2"):
-        lax.fori_loop(8, 16, first, 0)
+        lax.fori_loop(8, 16, first, 0, unroll=2)
     meet(2)
 
     tan2 = tans[0, 2]
@@ -281,7 +281,7 @@
             return carry
 
         with scope(f"blocks_{k}"):
-            lax.fori_loop(0, 16, blocks, 0)
+            lax.fori_loop(0, 16, blocks, 0, unroll=2)
         with scope(f"send_f{k}"):
             send_all(mixed, lambda i: fwd.at[k, i], mid.at[k, me], sends.at[k], recvs.at[k])
         mid[k, me] = fwd[k, me]
@@ -326,9 +326,9 @@
             return carry
 
         with scope(f"mid_{k}"):
-            lax.fori_loop(0, 16, lanes_1, 0)
-            lax.fori_loop(0, 16, banks, 0)
-            lax.fori_loop(0, 8, lanes_2, 0)
+            lax.fori_loop(0, 16, lanes_1, 0, unroll=2)
+            lax.fori_loop(0, 16, banks, 0, unroll=2)
+            lax.fori_loop(0, 8, lanes_2, 0, unroll=2)
         with scope(f"send_b{k}"):
             if k == 0:
                 send_all(mixed, lambda i: back.at[0, i], fin.at[me], sends.at[2], recvs.at[2])
@@ -361,7 +361,7 @@
                         half_done[b * 8 + r] = tiles[b]
                 return carry
 
-            lax.fori_loop(0, 8, last, 0)
+            lax.fori_loop(0, 8, last, 0, unroll=2)
     with scope("wait_b10"):
         wait_bytes(fin_1.at[pl.ds(0, N_DEV - 1)], recvs.at[3])
     with scope("last_10"):
@@ -371,7 +371,7 @@
             home_blocks(lambda d: fin_1[d], lambda d: fin[d, 0], done, r, tan_out)
             return carry
 
-        lax.fori_loop(0, 8, last_0, 0)
+        lax.fori_loop(0, 8, last_0, 0, unroll=2)
     with scope("wait_b11"):
         wait_bytes(raw.at[pl.ds(0, N_DEV - 1)], recvs.at[4])
 

time: 69.7 us -> 69.4 us (level)
  no operation moved by 1% of the time
where the time goes in v5:
time: 69.4 us; the launch traced here: 69.3 us
  Pallas kernels  69.3 us (100%)
    pallas_call x1, Pallas kernels, body(): pl.pallas_call(kernel, out_shape=(pltpu.VMEM((16, 8, 2, 8, 128), f32), pl...  68 us

profile of v5, /device:TPU:1, one launch (start us, length us, event | category | flops | bytes accessed | tf_op | source)
XLA Modules:
  0.0 69.3 jit_solution(8100334195525992460)
XLA Ops:
  0.0 68.0 %register.1 = (f32[16,8,2,8,128]{4,3,2,1,0:T(8,128)S(1)}, f32[128,8,128]{2,1,0:T(8,128)S(1)}, f32[128,8,128]{2,1,0:T(8,128)S(1)}, f32[2,8,128]{2,1,0:T(8,128)S(1)}) custom-call(f32[2,128,2,8,128]{4,3,2,1,0:T(8,128)} %bitcast.3, f32[128,2,8,128]{3,2,1,0:T(8,128)} %bitcast.4, f32[2,128]{1,0:T(2,128)} %diag_any.1, f32[2,4]{1,0:T(2,128)} %turn_any.1), custom_call_target="tpu_custom_call" | custom-call | tf_op jit(solution)/shard_map/register/pallas_call | solution.py:391
  68.0 1.4 %finish.1 = f32[2,16,8,2,8,128]{5,4,3,2,1,0:T(8,128)} custom-call(f32[16,8,2,8,128]{4,3,2,1,0:T(8,128)S(1)} %get-tuple-element.9.done, f32[128,8,128]{2,1,0:T(8,128)S(1)} %get-tuple-element.10.half_done, f32[128,8,128]{2,1,0:T(8,128)S(1)} %get-tuple-element.11.raw, f32[2,8,128]{2,1,0:T(8,128)S(1)} %get-tuple-element.12.tan), custom_call_target="tpu_custom_call" | custom-call | tf_op jit(solution)/shard_map/finish/pallas_call | solution.py:435

commit v6 on v5

--- a/solution.py
+++ b/solution.py
@@ -26,7 +26,7 @@
 )
 
 
-MIXED = sorted(STEPS, key=lambda s: (s[0] * 29 + s[1] * 53 + s[2] * 17 + s[3] * 71) * 37 % 127)
+MIXED = sorted(STEPS, key=lambda s: (s[0] * 45 + s[1] * 91 + s[2] * 23 + s[3] * 103) * 61 % 127)
 
 
 def lines(step):
@@ -166,30 +166,31 @@
         dst[b, r, 1] = v + tan[0] * u
 
 
-def finish(done, half_done, raw, tan, out, rows, stage, sems):
-    copies = [pltpu.make_async_copy(done.at[pl.ds(i * 4, 4)], out.at[0, pl.ds(i * 4, 4)], sems.at[i]) for i in range(4)]
-    for copy in copies:
-        copy.start()
-    home_rows(raw, rows, tan)
-    for r in range(8):
-        home_blocks(lambda d: rows[d], lambda d: half_done[d], stage, r, tan)
-        if r % 2:
-            copies.append(pltpu.make_async_copy(stage.at[:, pl.ds(r - 1, 2)], out.at[1, :, pl.ds(r - 1, 2)], sems.at[4 + r // 2]))
-            copies[-1].start()
+def finish(early, raw, tan, out, rows, stage, sems):
+    copies = []
+    for part in range(2):
+        home_rows(raw.at[:, part], rows, tan)
+        for r in range(8):
+            home_blocks(lambda d: rows[d], lambda d: early[d, part], stage.at[part], r, tan)
+            if r % 2:
+                at = pl.ds(r - 1, 2)
+                copies.append(
+                    pltpu.make_async_copy(stage.at[part, :, at], out.at[part, :, at], sems.at[part, r // 2])
+                )
+                copies[-1].start()
     for copy in copies:
         copy.wait()
 
 
-def kernel(amp, energy, diag_any, turn_any, done, half_done, raw, tan_out, diag, turn, a_in, e_in, e_rx, relay, fwd, mid, back, fin, fin_1, tables, tans, sems, sends, recvs, met):
+def kernel(amp, energy, diag_any, turn_any, early, raw, tan_out, diag, turn, a_in, e_in, e_rx, relay, fwd, mid, back, fin, tables, tans, sems, sends, recvs, met):
     bank, lane = place()
     me = bank * N_LANE + lane
     scope = jax.named_scope
-    late = [fin_1, raw]
 
     get_e = pltpu.make_async_copy(energy, e_in, sems.at[0])
     get_a = pltpu.make_async_copy(amp, a_in, sems.at[1])
     small = [pltpu.make_async_copy(diag_any, diag, sems.at[2]), pltpu.make_async_copy(turn_any, turn, sems.at[3])]
-    for get in [get_e, *small, get_a]:
+    for get in [get_e, *small]:
         get.start()
 
     spot = spots()
@@ -210,17 +211,18 @@
 
     def send_e(n):
         some = [spot(step) for step in MIXED if lines(step) == n]
-        send_all(some, lambda i: e_in.at[i], e_rx.at[me], sends.at[5], recvs.at[5])
+        send_all(some, lambda i: e_in.at[i], e_rx.at[me], sends.at[4], recvs.at[4])
 
     signal(0)
     with scope("wait_in"):
         get_e.wait()
+    get_a.start()
     meet(0)
     with scope("send_e0"):
         send_e(1)
         for j, (step, line) in enumerate(RELAYED):
             device, _ = spot(along(step, line)[0])
-            send(e_in.at[spot(step)[1]], relay.at[j], device, sends.at[5], recvs.at[6])
+            send(e_in.at[spot(step)[1]], relay.at[j], device, sends.at[4], recvs.at[5])
     e_rx[me] = e_in[me]
 
     with scope("tables"):
@@ -261,11 +263,11 @@
     with scope("first_1"):
         lax.fori_loop(4, 8, first, 0, unroll=2)
     with scope("wait_r"):
-        wait_bytes(relay, recvs.at[6])
+        wait_bytes(relay, recvs.at[5])
     with scope("relay"):
         for j, (step, line) in enumerate(RELAYED):
             part, rest = along(step, line)
-            send(relay.at[j], e_rx.at[spot(reverse(part))[1]], spot(rest)[0], sends.at[6], recvs.at[5])
+            send(relay.at[j], e_rx.at[spot(reverse(part))[1]], spot(rest)[0], sends.at[5], recvs.at[4])
     with scope("first_2"):
         lax.fori_loop(8, 16, first, 0, unroll=2)
     meet(2)
@@ -283,11 +285,11 @@
         with scope(f"blocks_{k}"):
             lax.fori_loop(0, 16, blocks, 0, unroll=2)
         with scope(f"send_f{k}"):
-            send_all(mixed, lambda i: fwd.at[k, i], mid.at[k, me], sends.at[k], recvs.at[k])
+            send_all(devices if k == 0 else mixed, lambda i: fwd.at[k, i], mid.at[k, me], sends.at[k], recvs.at[k])
         mid[k, me] = fwd[k, me]
 
     with scope("wait_e"):
-        wait_bytes(e_rx.at[pl.ds(0, N_DEV - 1)], recvs.at[5])
+        wait_bytes(e_rx.at[pl.ds(0, N_DEV - 1)], recvs.at[4])
     for k in range(2):
         with scope(f"wait_m{k}"):
             wait_bytes(mid.at[k, pl.ds(0, N_DEV - 1)], recvs.at[k])
@@ -329,20 +331,16 @@
             lax.fori_loop(0, 16, lanes_1, 0, unroll=2)
             lax.fori_loop(0, 16, banks, 0, unroll=2)
             lax.fori_loop(0, 8, lanes_2, 0, unroll=2)
+        home = fin if k == 0 else raw
         with scope(f"send_b{k}"):
-            if k == 0:
-                send_all(mixed, lambda i: back.at[0, i], fin.at[me], sends.at[2], recvs.at[2])
-            else:
-                for part in range(2):
-                    n = 3 + part
-                    send_all(
-                        devices, lambda i: back.at[1, i, part], late[part].at[me], sends.at[n], recvs.at[n]
-                    )
-        if k == 0:
-            fin[me] = back[0, me]
-        else:
-            for part in range(2):
-                late[part][me] = back[1, me, part]
+            send_all(
+                mixed if k == 0 else devices,
+                lambda i: back.at[k, i],
+                home.at[me],
+                sends.at[2 + k],
+                recvs.at[2 + k],
+            )
+        home[me] = back[k, me]
 
     with scope("wait_b0"):
         wait_bytes(fin.at[pl.ds(0, N_DEV - 1)], recvs.at[2])
@@ -355,49 +353,32 @@
             def last(r, carry):
                 tiles = butterfly([fin[b * 8 + r, part] for b in range(16)], tan_out[1])
                 for b in range(16):
-                    if part == 0:
-                        fin[b * 8 + r, 0] = tiles[b]
-                    else:
-                        half_done[b * 8 + r] = tiles[b]
+                    early[b * 8 + r, part] = tiles[b]
                 return carry
 
             lax.fori_loop(0, 8, last, 0, unroll=2)
-    with scope("wait_b10"):
-        wait_bytes(fin_1.at[pl.ds(0, N_DEV - 1)], recvs.at[3])
-    with scope("last_10"):
-        home_rows(fin_1, fin_1, tan_out)
-
-        def last_0(r, carry):
-            home_blocks(lambda d: fin_1[d], lambda d: fin[d, 0], done, r, tan_out)
-            return carry
-
-        lax.fori_loop(0, 8, last_0, 0, unroll=2)
-    with scope("wait_b11"):
-        wait_bytes(raw.at[pl.ds(0, N_DEV - 1)], recvs.at[4])
-
-    wait_bytes(e_in.at[pl.ds(0, N_DEV - 1)], sends.at[5])
-    wait_bytes(relay, sends.at[6])
+    wait_bytes(e_in.at[pl.ds(0, N_DEV - 1)], sends.at[4])
+    wait_bytes(relay, sends.at[5])
     for k in range(2):
         wait_bytes(fwd.at[k, pl.ds(0, N_DEV - 1)], sends.at[k])
-    wait_bytes(back.at[0, pl.ds(0, N_DEV - 1)], sends.at[2])
-    for part in range(2):
-        wait_bytes(back.at[1, pl.ds(0, N_DEV - 1), part], sends.at[3 + part])
+        wait_bytes(back.at[k, pl.ds(0, N_DEV - 1)], sends.at[2 + k])
+    with scope("wait_b1"):
+        wait_bytes(raw.at[pl.ds(0, N_DEV - 1)], recvs.at[3])
 
 
 def body(amplitudes, energies, diagonal_angles, turn_angles):
     f32 = jnp.float32
     anywhere = pl.BlockSpec(memory_space=pl.ANY)
     vmem = pl.BlockSpec(memory_space=pltpu.VMEM)
-    done, half_done, raw, tan = pl.pallas_call(
+    early, raw, tan = pl.pallas_call(
         kernel,
         out_shape=(
-            pltpu.VMEM((16, 8, 2, 8, 128), f32),
-            pltpu.VMEM((N_DEV, 8, 128), f32),
-            pltpu.VMEM((N_DEV, 8, 128), f32),
+            pltpu.VMEM((N_DEV, 2, 8, 128), f32),
+            pltpu.VMEM((N_DEV, 2, 8, 128), f32),
             pltpu.VMEM((2, 8, 128), f32),
         ),
         in_specs=[anywhere] * 4,
-        out_specs=(vmem,) * 4,
+        out_specs=(vmem,) * 3,
         scratch_shapes=[
             pltpu.VMEM((2, 128), f32),
             pltpu.VMEM((2, 4), f32),
@@ -409,12 +390,11 @@
             pltpu.VMEM((2, N_DEV, 2, 8, 128), f32),
             pltpu.VMEM((2, N_DEV, 2, 8, 128), f32),
             pltpu.VMEM((N_DEV, 2, 8, 128), f32),
-            pltpu.VMEM((N_DEV, 8, 128), f32),
             pltpu.VMEM((2, 256, 256), jnp.bfloat16),
             pltpu.VMEM((2, 4, 8, 128), f32),
             pltpu.SemaphoreType.DMA((4,)),
-            pltpu.SemaphoreType.DMA((7,)),
-            pltpu.SemaphoreType.DMA((7,)),
+            pltpu.SemaphoreType.DMA((6,)),
+            pltpu.SemaphoreType.DMA((6,)),
             pltpu.SemaphoreType.REGULAR((2,)),
         ],
         compiler_params=pltpu.CompilerParams(
@@ -435,16 +415,16 @@
     out = pl.pallas_call(
         finish,
         out_shape=jax.ShapeDtypeStruct((2, 16, 8, 2, 8, 128), f32),
-        in_specs=[vmem] * 4,
+        in_specs=[vmem] * 3,
         out_specs=anywhere,
         scratch_shapes=[
             pltpu.VMEM((N_DEV, 8, 128), f32),
-            pltpu.VMEM((16, 8, 2, 8, 128), f32),
-            pltpu.SemaphoreType.DMA((8,)),
+            pltpu.VMEM((2, 16, 8, 2, 8, 128), f32),
+            pltpu.SemaphoreType.DMA((2, 4)),
         ],
         compiler_params=pltpu.CompilerParams(vmem_limit_bytes=8 * 1024 * 1024),
         name="finish",
-    )(done, half_done, raw, tan)
+    )(early, raw, tan)
     return out.reshape(2, 16, 128, 128)
 
 

time: 69.4 us -> 69.1 us (level)
  no operation moved by 1% of the time
where the time goes in v6:
time: 69.1 us; the launch traced here: 69 us
  Pallas kernels  69 us (100%)
    pallas_call x1, Pallas kernels, body(): pl.pallas_call(kernel, out_shape=(pltpu.VMEM((N_DEV, 2, 8, 128), f32), pl...  67.4 us
    pallas_call x1, Pallas kernels, body(): pl.pallas_call(finish, out_shape=jax.ShapeDtypeStruct((2, 16, 8, 2, 8, 12...  1.56 us

profile of v6, /device:TPU:1, one launch (start us, length us, event | category | flops | bytes accessed | tf_op | source)
XLA Modules:
  0.0 69.0 jit_solution(4587475309849641431)
XLA Ops:
  0.0 67.4 %register.1 = (f32[128,2,8,128]{3,2,1,0:T(8,128)S(1)}, f32[128,2,8,128]{3,2,1,0:T(8,128)S(1)}, f32[2,8,128]{2,1,0:T(8,128)S(1)}) custom-call(f32[2,128,2,8,128]{4,3,2,1,0:T(8,128)} %bitcast.3, f32[128,2,8,128]{3,2,1,0:T(8,128)} %bitcast.4, f32[2,128]{1,0:T(2,128)} %diag_any.1, f32[2,4]{1,0:T(2,128)} %turn_any.1), custom_call_target="tpu_custom_call" | custom-call | tf_op jit(solution)/shard_map/register/pallas_call | solution.py:373
  67.4 1.6 %finish.1 = f32[2,16,8,2,8,128]{5,4,3,2,1,0:T(8,128)} custom-call(f32[128,2,8,128]{3,2,1,0:T(8,128)S(1)} %get-tuple-element.8.early, f32[128,2,8,128]{3,2,1,0:T(8,128)S(1)} %get-tuple-element.9.raw, f32[2,8,128]{2,1,0:T(8,128)S(1)} %get-tuple-element.10.tan), custom_call_target="tpu_custom_call" | custom-call | tf_op jit(solution)/shard_map/finish/pallas_call | solution.py:415

commit v7 on v6

--- a/solution.py
+++ b/solution.py
@@ -26,7 +26,7 @@
 )
 
 
-MIXED = sorted(STEPS, key=lambda s: (s[0] * 45 + s[1] * 91 + s[2] * 23 + s[3] * 103) * 61 % 127)
+MIXED = sorted(STEPS, key=lambda s: (s[0] * 11 + s[1] * 67 + s[2] * 83 + s[3] * 31) * 43 % 127)
 
 
 def lines(step):

time: 69.1 us -> 68.8 us (level)
  no operation moved by 1% of the time
where the time goes in v7:
time: 68.8 us; the launch traced here: 68.6 us
  Pallas kernels  68.6 us (100%)
    pallas_call x1, Pallas kernels, body(): pl.pallas_call(kernel, out_shape=(pltpu.VMEM((N_DEV, 2, 8, 128), f32), pl...  67.1 us
    pallas_call x1, Pallas kernels, body(): pl.pallas_call(finish, out_shape=jax.ShapeDtypeStruct((2, 16, 8, 2, 8, 12...  1.56 us

profile of v7, /device:TPU:1, one launch (start us, length us, event | category | flops | bytes accessed | tf_op | source)
XLA Modules:
  0.0 68.6 jit_solution(9241295578478703056)
XLA Ops:
  0.0 67.1 %register.1 = (f32[128,2,8,128]{3,2,1,0:T(8,128)S(1)}, f32[128,2,8,128]{3,2,1,0:T(8,128)S(1)}, f32[2,8,128]{2,1,0:T(8,128)S(1)}) custom-call(f32[2,128,2,8,128]{4,3,2,1,0:T(8,128)} %bitcast.3, f32[128,2,8,128]{3,2,1,0:T(8,128)} %bitcast.4, f32[2,128]{1,0:T(2,128)} %diag_any.1, f32[2,4]{1,0:T(2,128)} %turn_any.1), custom_call_target="tpu_custom_call" | custom-call | tf_op jit(solution)/shard_map/register/pallas_call | solution.py:373
  67.1 1.6 %finish.1 = f32[2,16,8,2,8,128]{5,4,3,2,1,0:T(8,128)} custom-call(f32[128,2,8,128]{3,2,1,0:T(8,128)S(1)} %get-tuple-element.8.early, f32[128,2,8,128]{3,2,1,0:T(8,128)S(1)} %get-tuple-element.9.raw, f32[2,8,128]{2,1,0:T(8,128)S(1)} %get-tuple-element.10.tan), custom_call_target="tpu_custom_call" | custom-call | tf_op jit(solution)/shard_map/finish/pallas_call | solution.py:415

commit v8 on v7

--- a/solution.py
+++ b/solution.py
@@ -328,9 +328,9 @@
             return carry
 
         with scope(f"mid_{k}"):
-            lax.fori_loop(0, 16, lanes_1, 0, unroll=2)
-            lax.fori_loop(0, 16, banks, 0, unroll=2)
-            lax.fori_loop(0, 8, lanes_2, 0, unroll=2)
+            lax.fori_loop(0, 16, lanes_1, 0, unroll=4)
+            lax.fori_loop(0, 16, banks, 0, unroll=4)
+            lax.fori_loop(0, 8, lanes_2, 0, unroll=4)
         home = fin if k == 0 else raw
         with scope(f"send_b{k}"):
             send_all(

time: 68.8 us -> 68.6 us (level)
  no operation moved by 1% of the time
where the time goes in v8:
time: 68.6 us; the launch traced here: 68.5 us
  Pallas kernels  68.5 us (100%)
    pallas_call x1, Pallas kernels, body(): pl.pallas_call(kernel, out_shape=(pltpu.VMEM((N_DEV, 2, 8, 128), f32), pl...  66.9 us
    pallas_call x1, Pallas kernels, body(): pl.pallas_call(finish, out_shape=jax.ShapeDtypeStruct((2, 16, 8, 2, 8, 12...  1.56 us

profile of v8, /device:TPU:1, one launch (start us, length us, event | category | flops | bytes accessed | tf_op | source)
XLA Modules:
  0.0 68.5 jit_solution(17362593883737530283)
XLA Ops:
  0.0 66.9 %register.1 = (f32[128,2,8,128]{3,2,1,0:T(8,128)S(1)}, f32[128,2,8,128]{3,2,1,0:T(8,128)S(1)}, f32[2,8,128]{2,1,0:T(8,128)S(1)}) custom-call(f32[2,128,2,8,128]{4,3,2,1,0:T(8,128)} %bitcast.3, f32[128,2,8,128]{3,2,1,0:T(8,128)} %bitcast.4, f32[2,128]{1,0:T(2,128)} %diag_any.1, f32[2,4]{1,0:T(2,128)} %turn_any.1), custom_call_target="tpu_custom_call" | custom-call | tf_op jit(solution)/shard_map/register/pallas_call | solution.py:373
  66.9 1.6 %finish.1 = f32[2,16,8,2,8,128]{5,4,3,2,1,0:T(8,128)} custom-call(f32[128,2,8,128]{3,2,1,0:T(8,128)S(1)} %get-tuple-element.8.early, f32[128,2,8,128]{3,2,1,0:T(8,128)S(1)} %get-tuple-element.9.raw, f32[2,8,128]{2,1,0:T(8,128)S(1)} %get-tuple-element.10.tan), custom_call_target="tpu_custom_call" | custom-call | tf_op jit(solution)/shard_map/finish/pallas_call | solution.py:415
